TPU v7x, 32 devices: a whole 2x2x4 slice. The times are simulated.
32 devices in a mesh: seq: 16 (over z, y, core), slide: 2 (over x).
Axes of the slice: x: 2, y: 2, z: 4, core: 2. Of those that a mesh axis runs over, the one named last changes fastest.
Arguments:
- layer_input: bfloat16 [2, 4096, 768], P('slide', 'seq'), may hold values from -6 to 6
- cotangent: bfloat16 [2, 4096, 768], P('slide', 'seq'), may hold values from -6 to 6
- layer_norm_gain: float32 [768], replicated, may hold values from 0.25 to 1.75
- layer_norm_bias: float32 [768], replicated, may hold values from -3 to 3
- query_key_value_weight: bfloat16 [768, 2304], replicated, may hold values from -4 to 4
- output_weight: bfloat16 [768, 768], replicated, may hold values from -0.21875 to 0.21875
Outputs:
- layer_output: bfloat16 [2, 4096, 768], P('slide', 'seq')
- input_grad: bfloat16 [2, 4096, 768], P('slide', 'seq')
- grad_qkv: float32 [768, 2304], P('seq')
- grad_out: float32 [768, 768], P('seq')
- grad_gain: float32 [768], replicated
- grad_bias: float32 [768], replicated
All inputs are finite; a program needn't handle non-finite values.
Results may differ from a plain program's by a relative error of at most 0.011.
Values may be sent and summed in bfloat16 or wider, within the bound.
A program may use at most 128 MiB of HBM per device.

v0:
```python
import jax
import jax.numpy as jnp
from jax import lax
from jax.sharding import PartitionSpec as P

HEADS = 12
EPS = 1e-05


def from_behind(block, axis, distance):
    devices = range(lax.axis_size(axis))
    route = [(i - distance, i) for i in devices if i - distance in devices]
    return lax.ppermute(block, axis, route)


def apply_layer_norm(token_rows, scale_gain, shift_bias):
    values = token_rows.astype(jnp.float32)
    centered_rows = values - jnp.mean(values, axis=-1, keepdims=True)
    inverse_deviation = lax.rsqrt(
        jnp.mean(centered_rows * centered_rows, axis=-1, keepdims=True) + EPS
    )
    normalized_rows = centered_rows * inverse_deviation
    return (
        (normalized_rows * scale_gain + shift_bias).astype(jnp.bfloat16),
        normalized_rows,
        inverse_deviation,
    )


def attend(qkv_self, memory_key_value, memory_present):
    token_length = qkv_self.shape[0]
    feature_width = memory_key_value.shape[1] // 2
    head_dim = feature_width // HEADS
    query = qkv_self[:, :feature_width].reshape(token_length, HEADS, head_dim)
    keys = jnp.concatenate(
        [memory_key_value[:, :feature_width], qkv_self[:, feature_width : 2 * feature_width]], 0
    ).reshape(2 * token_length, HEADS, head_dim)
    values = jnp.concatenate(
        [memory_key_value[:, feature_width:], qkv_self[:, 2 * feature_width :]], 0
    ).reshape(2 * token_length, HEADS, head_dim)
    scores = jnp.einsum(
        "qhe,khe->hqk", query, keys, preferred_element_type=jnp.float32
    ) * head_dim ** (-0.5)
    row_ids = lax.broadcasted_iota(jnp.int32, (token_length, 2 * token_length), 0)
    col_ids = lax.broadcasted_iota(jnp.int32, (token_length, 2 * token_length), 1)
    allowed = jnp.where(col_ids < token_length, memory_present, col_ids - token_length <= row_ids)
    scores = jnp.where(allowed[None], scores, -1e30)
    top = jnp.max(scores, axis=-1, keepdims=True)
    weights = jnp.exp(scores - top)
    probs = weights / jnp.sum(weights, axis=-1, keepdims=True)
    probs_b = probs.astype(jnp.bfloat16)
    mixed = jnp.einsum("hqk,khe->qhe", probs_b, values, preferred_element_type=jnp.float32)
    mixed = mixed.reshape(token_length, feature_width).astype(jnp.bfloat16)
    return (mixed, probs, probs_b, query, keys, values)


def attend_back(d_mixed, probs, probs_b, query, keys, values):
    token_length, heads, head_dim = query.shape
    grad_heads = d_mixed.reshape(token_length, heads, head_dim)
    d_probs = jnp.einsum("qhe,khe->hqk", grad_heads, values, preferred_element_type=jnp.float32)
    d_scores = probs * (d_probs - jnp.sum(d_probs * probs, axis=-1, keepdims=True))
    d_scores_b = (d_scores * head_dim ** (-0.5)).astype(jnp.bfloat16)
    d_query = jnp.einsum("hqk,khe->qhe", d_scores_b, keys, preferred_element_type=jnp.float32)
    d_keys = jnp.einsum("hqk,qhe->khe", d_scores_b, query, preferred_element_type=jnp.float32)
    d_values = jnp.einsum("hqk,qhe->khe", probs_b, grad_heads, preferred_element_type=jnp.float32)
    return (
        d_query.reshape(token_length, -1).astype(jnp.bfloat16),
        d_keys.reshape(2 * token_length, -1).astype(jnp.bfloat16),
        d_values.reshape(2 * token_length, -1).astype(jnp.bfloat16),
    )


def block_forward(
    token_rows,
    gradient_list,
    current_query_key_value,
    memory_key_value,
    memory_present,
    current_normed,
    current_normalized,
    current_inverse_deviation,
    query_key_value_weight,
    output_weight,
    scale_gain,
):
    token_length = token_rows.shape[0]
    mixed, probs, probs_b, query, keys, values = attend(
        current_query_key_value, memory_key_value, memory_present
    )
    block_output = (
        token_rows.astype(jnp.float32)
        + jnp.dot(mixed, output_weight, preferred_element_type=jnp.float32)
    ).astype(jnp.bfloat16)
    d_mixed = jnp.dot(gradient_list, output_weight.T, preferred_element_type=jnp.float32).astype(
        jnp.bfloat16
    )
    grad_wout = jnp.dot(mixed.T, gradient_list, preferred_element_type=jnp.float32)
    d_query, d_keys, d_values = attend_back(d_mixed, probs, probs_b, query, keys, values)
    d_own = jnp.concatenate([d_query, d_keys[token_length:], d_values[token_length:]], 1)
    memory_gradient = jnp.concatenate([d_keys[:token_length], d_values[:token_length]], 1)
    grad_wqkv = jnp.dot(current_normed.T, d_own, preferred_element_type=jnp.float32)
    normed_gradient = jnp.dot(d_own, query_key_value_weight.T, preferred_element_type=jnp.float32)
    gain_gradient = jnp.sum(normed_gradient * current_normalized, axis=0)
    grad_b = jnp.sum(normed_gradient, axis=0)
    normalized_gradient = normed_gradient * scale_gain
    row_gradient = current_inverse_deviation * (
        normalized_gradient
        - jnp.mean(normalized_gradient, axis=-1, keepdims=True)
        - current_normalized
        * jnp.mean(normalized_gradient * current_normalized, axis=-1, keepdims=True)
    )
    input_gradient = (gradient_list.astype(jnp.float32) + row_gradient).astype(jnp.bfloat16)
    return (
        block_output,
        input_gradient,
        memory_gradient,
        (grad_wqkv, grad_wout, gain_gradient, grad_b),
    )


def memory_contributions(prior_normed, prior_normalized, memory_gradient, query_key_value_weight):
    feature_width = prior_normed.shape[1]
    key_value_gradient = jnp.dot(
        prior_normed.T, memory_gradient, preferred_element_type=jnp.float32
    )
    normed_gradient = jnp.dot(
        memory_gradient,
        query_key_value_weight[:, feature_width:].T,
        preferred_element_type=jnp.float32,
    )
    return (
        key_value_gradient,
        jnp.sum(normed_gradient * prior_normalized, axis=0),
        jnp.sum(normed_gradient, axis=0),
    )


def on_device(
    layer_input, cotangent, layer_norm_gain, layer_norm_bias, query_key_value_weight, output_weight
):
    token_rows = layer_input[0]
    gradient_list = cotangent[0]
    feature_width = token_rows.shape[1]
    normed_rows, normalized_rows, inverse_deviation = apply_layer_norm(
        token_rows, layer_norm_gain, layer_norm_bias
    )
    query_key_value = jnp.dot(
        normed_rows, query_key_value_weight, preferred_element_type=jnp.float32
    ).astype(jnp.bfloat16)
    has_first = lax.axis_index("seq") > 0
    previous_token_rows = from_behind(token_rows, "seq", 1)
    previous_normed_rows, previous_normalized, ignored_value = apply_layer_norm(
        previous_token_rows, layer_norm_gain, layer_norm_bias
    )
    kv_before = jnp.dot(
        previous_normed_rows,
        query_key_value_weight[:, feature_width:],
        preferred_element_type=jnp.float32,
    ).astype(jnp.bfloat16)
    block_output, input_gradient, memory_gradient, term_list = block_forward(
        token_rows,
        gradient_list,
        query_key_value,
        kv_before,
        has_first,
        normed_rows,
        normalized_rows,
        inverse_deviation,
        query_key_value_weight,
        output_weight,
        layer_norm_gain,
    )
    acc_qkv = term_list[0]
    acc_out = term_list[1]
    acc_gain = term_list[2]
    acc_bias = term_list[3]
    key_value_gradient, memory_gain, memory_bias = memory_contributions(
        previous_normed_rows, previous_normalized, memory_gradient, query_key_value_weight
    )
    acc_gain = acc_gain + memory_gain
    acc_bias = acc_bias + memory_bias
    combined = jnp.concatenate(
        [acc_qkv[:, :feature_width], acc_qkv[:, feature_width:] + key_value_gradient, acc_out], 1
    )
    seq_count = lax.axis_size("seq")
    slide_count = lax.axis_size("slide")
    factor = 1.0 / float(seq_count * slide_count * token_rows.shape[0]) ** 0.5
    gain_sum, bias_sum = lax.psum((acc_gain, acc_bias), ("seq", "slide"))
    shard = lax.psum_scatter(combined, "seq", scatter_dimension=0, tiled=True)
    shard = lax.psum(shard.astype(jnp.bfloat16), "slide").astype(jnp.float32)
    shard = shard * factor
    layer_output = block_output[None]
    input_grad = input_gradient[None]
    return (
        layer_output,
        input_grad,
        shard[:, : 3 * feature_width],
        shard[:, 3 * feature_width :],
        gain_sum * factor,
        bias_sum * factor,
    )


def solution(mesh):
    placed = (P("slide", "seq", None), P("slide", "seq", None), P(), P(), P(), P())
    return jax.shard_map(
        on_device,
        mesh=mesh,
        in_specs=placed,
        out_specs=(
            P("slide", "seq", None),
            P("slide", "seq", None),
            P("seq", None),
            P("seq", None),
            P(),
            P(),
        ),
        check_vma=False,
    )
```

profile of v0, /device:TPU:0, one launch (start us, length us, event | category | flops | bytes accessed | tf_op | source)
XLA Modules:
  0.0 261.9 jit_solution(17593352173310648972)
XLA Ops:
  7.2 0.0 reduce-scatter.2.cloned.1.call-start
  7.2 2.6 collective-permute-start
  9.8 1.1 convert_reduce_fusion
  10.9 1.2 fusion.65
  12.2 3.4 %convolution_convert_fusion = bf16[256,2304]{1,0:T(8,128)(2,1)S(1)} fusion(bf16[768,2304]{1,0:T(8,128)(2,1)} %param.10, f32[256]{0:T(256)S(1)} %add_rsqrt_fusion, f32[256]{0:T(256)S(1)} %broadcast_multiply_fusion.4, f32[768]{0:T(1024)} %param.9, f32[768]{0:T(1024)} %param.8, bf16[1,256,768]{2,1,0:T(8,128)(2,1)} %param.6), kind=kOutput, calls=%fused_computation.10 | convolution fusion | flops 907739136 | bytes 5120000 | tf_op jit(solution)/shard_map/dot_general | solution.py:147
  15.6 0.1 fusion.91
  15.7 1.3 convolution_convert_fusion.2
  17.0 0.5 iota_compare_fusion.1
  17.5 1.2 copy.24
  18.6 0.9 copy.22
  19.6 1.4 fusion.69
  21.0 0.1 convert_reduce_fusion.1
  21.1 0.2 fusion.66
  21.4 2.5 convolution_convert_fusion.1
  24.0 0.1 fusion.94
  24.0 1.3 pad_maximum_fusion.2
  25.3 1.4 copy.21
  26.7 2.3 copy.23
  29.0 6.7 %fusion.95 = (f32[12,256]{1,0:T(8,128)}, f32[12,256,512]{2,1,0:T(8,128)}) fusion(pred[256,512]{1,0:T(8,128)(4,1)} %fusion.69, bf16[256,12,64]{0,2,1:T(8,128)(2,1)S(1)} %bitcast.71, bf16[512,12,64]{0,2,1:T(8,128)(2,1)} %bitcast.69), kind=kOutput, calls=%fused_computation.104 | convolution fusion | flops 207618560 | bytes 7614464 | tf_op jit(solution)/shard_map/sub | solution.py:49
  35.7 4.1 %fusion.37 = bf16[12,64,256]{2,1,0:T(8,128)(2,1)S(1)} fusion(bf16[512,12,64]{0,2,1:T(8,128)(2,1)S(1)} %bitcast.55, f32[12,256,512]{2,1,0:T(8,128)} %get-tuple-element.24, f32[12,256]{1,0:T(8,128)} %get-tuple-element.23), kind=kOutput, calls=%fused_computation.33 | convolution fusion | flops 204668928 | bytes 7483392 | tf_op jit(solution)/shard_map/hqk,khe->qhe/dot_general | solution.py:52
  39.8 0.5 copy-done.20
  40.3 1.7 fusion.30
  42.1 3.7 %fusion.96 = f32[12,256,512]{2,1,0:T(8,128)} fusion(bf16[256,12,64]{0,2,1:T(8,128)(2,1)S(1)} %bitcast.58, bf16[512,12,64]{0,2,1:T(8,128)(2,1)S(1)} %bitcast.56), kind=kOutput, calls=%fused_computation.105 | convolution fusion | flops 201326592 | bytes 7471104 | tf_op jit(solution)/shard_map/qhe,khe->hqk/dot_general | solution.py:60
  45.7 22.5 %fusion.40 = bf16[12,64,256]{2,1,0:T(8,128)(2,1)} fusion(bf16[512,12,64]{0,2,1:T(8,128)(2,1)} %bitcast.70, f32[12,256,512]{2,1,0:T(8,128)} %fusion.96, f32[12,256,512]{2,1,0:T(8,128)} %get-tuple-element.24, f32[12,256]{1,0:T(8,128)} %get-tuple-element.23), kind=kOutput, calls=%fused_computation.34 | convolution fusion | flops 212536832 | bytes 13774848 | tf_op jit(solution)/shard_map/hqk,khe->qhe/dot_general | solution.py:63
  68.2 25.9 %fusion.33 = bf16[512,12,64]{0,2,1:T(8,128)(2,1)} fusion(bf16[256,12,64]{0,2,1:T(8,128)(2,1)S(1)} %bitcast.72, f32[12,256,512]{2,1,0:T(8,128)} %fusion.96, f32[12,256,512]{2,1,0:T(8,128)} %get-tuple-element.24, f32[12,256]{1,0:T(8,128)S(1)} %copy-done.22), kind=kOutput, calls=%fused_computation.30 | convolution fusion | flops 212733440 | bytes 13774848 | tf_op jit(solution)/shard_map/hqk,qhe->khe/dot_general | solution.py:64
  94.1 1.3 fusion.93
  95.4 1.9 fusion.73
  97.3 0.1 fusion.92
  97.4 1.3 fusion.70
  98.8 1.6 slice.80
  100.4 3.3 %slice_add_fusion = f32[768,1536]{1,0:T(8,128)} fusion(f32[768,2304]{1,0:T(8,128)S(1)} %fusion.70, bf16[256,768]{0,1:T(8,128)(2,1)S(1)} %bitcast.59, bf16[256,768]{0,1:T(8,128)(2,1)S(1)} %bitcast.61, bf16[256,768]{1,0:T(8,128)(2,1)S(1)} %collective-permute-done, f32[768]{0:T(1024)S(1)} %copy-done.13, f32[768]{0:T(1024)S(1)} %copy-done.12, ...), kind=kOutput, calls=%fused_computation.9 | convolution fusion | flops 607911936 | bytes 10625024 | tf_op jit(solution)/shard_map/dot_general | solution.py:123
  103.6 8.7 %pad_maximum_fusion = f32[768,3072]{1,0:T(8,128)} fusion(f32[768,768]{1,0:T(8,128)} %fusion.73, f32[768,1536]{1,0:T(8,128)} %slice_add_fusion, f32[768,768]{1,0:T(8,128)} %slice.80), kind=kLoop, calls=%fused_computation.2 | loop fusion | flops 4718592 | bytes 18874368 | tf_op jit(solution)/shard_map/concatenate | solution.py:182
  112.4 0.0 all-reduce.3.cloned.1.call-start
  112.4 0.6 copy-done.16
  113.1 2.7 %fusion.90 = (f32[768]{0:T(1024)S(1)}, f32[768]{0:T(1024)S(1)}) fusion(f32[256]{0:T(256)} %copy-done.17, f32[256]{0:T(256)S(1)} %copy-done.16, bf16[256,768]{1,0:T(8,128)(2,1)S(1)} %collective-permute-done, bf16[768,2304]{1,0:T(8,128)(2,1)} %param.10, bf16[256,768]{0,1:T(8,128)(2,1)S(1)} %bitcast.60, bf16[256,768]{0,1:T(8,128)(2,1)S(1)} %bitcast.62), kind=kOutput, calls=%fused_computation.99 | convolution fusion | flops 606730752 | bytes 3547136 | tf_op jit(solution)/shard_map/dot_general | solution.py:126
  115.8 0.4 copy-done.19
  116.1 1.4 fusion.64
  117.6 43.3 %all-reduce = (f32[768]{0:T(1024)S(1)}, f32[768]{0:T(1024)S(1)}) all-reduce(f32[768]{0:T(1024)S(1)} %add.62, f32[768]{0:T(1024)S(1)} %add.63), channel_id=1, replica_groups=mesh['seq'=16,'slide'=2] {'seq','slide'}, use_global_device_ids=true, to_apply=%region_13.14 | all-reduce | flops 1536 | bytes 12288 | tf_op jit(solution)/shard_map/psum | solution.py:188
  160.9 0.6 broadcast_multiply_fusion.1
  161.5 0.6 broadcast_multiply_fusion
  162.1 64.4 %reduce-scatter.2.cloned.1.call-done = f32[48,3072]{1,0:T(8,128)} async-done(((f32[768,3072]{1,0:T(8,128)}), f32[48,3072]{1,0:T(8,128)}) %reduce-scatter.2.cloned.1.call-update) | async-done | bytes 589840 | tf_op jit(solution)/shard_map/reduce_scatter | solution.py:189
  226.4 1.8 convert_element_type.99
  228.2 1.3 fusion.43
  229.5 1.1 fusion.72
  230.6 22.1 %all-reduce.3.cloned.1.call-done = bf16[48,3072]{1,0:T(8,128)(2,1)} async-done(((bf16[48,3072]{1,0:T(8,128)(2,1)}), bf16[48,3072]{1,0:T(8,128)(2,1)}) %all-reduce.3.cloned.1.call-update) | async-done | bytes 294928 | tf_op jit(solution)/shard_map/psum | solution.py:190
  252.6 1.0 convert_multiply_fusion
  253.6 0.7 slice.85
  254.3 0.8 slice.84
  (55 shorter events, 0.2 us)
Async XLA Ops:
  7.2 8.5 %copy-start = (bf16[768,768]{1,0:T(8,128)(2,1)S(1)}, bf16[768,768]{1,0:T(8,128)(2,1)}, u32[]{:S(2)}) copy-start(bf16[768,768]{1,0:T(8,128)(2,1)} %param.11) | copy-start | bytes 3538948
  7.2 219.2 %reduce-scatter.2.cloned.1.call-start = ((), (), s32[]{:S(2)}) async-start(), calls=%async_computation.1 | async-start | bytes 10027008 | tf_op jit(solution)/shard_map/reduce_scatter | solution.py:189
  7.2 13.7 %collective-permute-start = (bf16[256,768]{1,0:T(8,128)(2,1)}, bf16[256,768]{1,0:T(8,128)(2,1)S(1)}, u32[]{:S(2)}, u32[]{:S(2)}) collective-permute-start(bf16[256,768]{1,0:T(8,128)(2,1)} %bitcast.54), channel_id=1, source_target_pairs={{0,2},{2,4},{4,6},{6,8},{8,10},{10,12},{12,14},{14,16},{16,18},{18... | collective-permute-start | bytes 1179656 | tf_op jit(solution)/shard_map/ppermute | solution.py:13
  12.2 3.5 %copy-start.2 = (bf16[1,256,768]{2,1,0:T(8,128)(2,1)S(1)}, bf16[1,256,768]{2,1,0:T(8,128)(2,1)}, u32[]{:S(2)}) copy-start(bf16[1,256,768]{2,1,0:T(8,128)(2,1)} %param.7) | copy-start | bytes 1179652
  15.6 5.8 %copy-start.12 = (f32[768]{0:T(1024)S(1)}, f32[768]{0:T(1024)}, u32[]{:S(2)}) copy-start(f32[768]{0:T(1024)} %param.8) | copy-start | bytes 9220
  15.6 5.8 %copy-start.13 = (f32[768]{0:T(1024)S(1)}, f32[768]{0:T(1024)}, u32[]{:S(2)}) copy-start(f32[768]{0:T(1024)} %param.9) | copy-start | bytes 9220
  21.1 2.8 %copy-start.14 = (f32[256]{0:T(256)}, f32[256]{0:T(256)S(1)}, u32[]{:S(2)}) copy-start(f32[256]{0:T(256)S(1)} %broadcast_multiply_fusion.5) | copy-start | bytes 3076
  21.4 2.6 copy-start.17
  24.0 5.0 %copy-start.8 = (bf16[256,768]{0,1:T(8,128)(2,1)S(1)}, bf16[256,768]{0,1:T(8,128)(2,1)}, u32[]{:S(2)}) copy-start(bf16[256,768]{0,1:T(8,128)(2,1)} %copy.22) | copy-start | bytes 1179652
  35.7 4.6 %copy-start.20 = (f32[12,256,512]{2,1,0:T(8,128)S(1)}, f32[12,256,512]{2,1,0:T(8,128)}, u32[]{:S(2)}) copy-start(f32[12,256,512]{2,1,0:T(8,128)} %get-tuple-element.24) | copy-start | bytes 18874372
  35.7 4.6 %copy-start.21 = (f32[12,256]{1,0:T(8,128)S(1)}, f32[12,256]{1,0:T(8,128)}, u32[]{:S(2)}) copy-start(f32[12,256]{1,0:T(8,128)} %get-tuple-element.23) | copy-start | bytes 36868
  45.7 22.5 %copy-start.9 = (bf16[256,768]{0,1:T(8,128)(2,1)S(1)}, bf16[256,768]{0,1:T(8,128)(2,1)}, u32[]{:S(2)}) copy-start(bf16[256,768]{0,1:T(8,128)(2,1)} %copy.22) | copy-start | bytes 1179652
  45.7 22.5 %copy-start.22 = (f32[12,256]{1,0:T(8,128)S(1)}, f32[12,256]{1,0:T(8,128)}, u32[]{:S(2)}) copy-start(f32[12,256]{1,0:T(8,128)} %get-tuple-element.23) | copy-start | bytes 36868
  94.1 3.2 %copy-start.7 = (bf16[512,12,64]{0,2,1:T(8,128)(2,1)S(1)}, bf16[512,12,64]{0,2,1:T(8,128)(2,1)}, u32[]{:S(2)}) copy-start(bf16[512,12,64]{0,2,1:T(8,128)(2,1)} %fusion.33) | copy-start | bytes 2359300
  94.1 3.3 %copy-start.1 = (bf16[1,256,768]{2,1,0:T(8,128)(2,1)S(1)}, bf16[1,256,768]{2,1,0:T(8,128)(2,1)}, u32[]{:S(2)}) copy-start(bf16[1,256,768]{2,1,0:T(8,128)(2,1)} %param.6) | copy-start | bytes 1179652
  94.1 3.3 %copy-start.10 = (bf16[12,64,256]{2,1,0:T(8,128)(2,1)S(1)}, bf16[12,64,256]{2,1,0:T(8,128)(2,1)}, u32[]{:S(2)}) copy-start(bf16[12,64,256]{2,1,0:T(8,128)(2,1)} %fusion.40) | copy-start | bytes 1179652
  95.4 3.3 %copy-start.3 = (bf16[256,12,64]{0,2,1:T(8,128)(2,1)}, bf16[256,12,64]{0,2,1:T(8,128)(2,1)S(1)}, u32[]{:S(2)}) copy-start(bf16[256,12,64]{0,2,1:T(8,128)(2,1)S(1)} %get-tuple-element.20) | copy-start | bytes 1179652
  97.4 1.4 copy-start.5
  98.8 1.6 copy-start.15
  98.8 1.6 copy-start.18
  112.4 0.7 copy-start.16
  112.4 140.2 %all-reduce.3.cloned.1.call-start = ((), (), s32[]{:S(2)}) async-start(), calls=%async_computation.2 | async-start | bytes 589824 | tf_op jit(solution)/shard_map/psum | solution.py:190
  113.0 2.7 %copy-start.4 = (bf16[256,12,64]{0,2,1:T(8,128)(2,1)S(1)}, bf16[256,12,64]{0,2,1:T(8,128)(2,1)}, u32[]{:S(2)}) copy-start(bf16[256,12,64]{0,2,1:T(8,128)(2,1)} %copy-done.3) | copy-start | bytes 1179652
  113.1 2.7 %copy-start.6 = (bf16[256,12,64]{0,2,1:T(8,128)(2,1)S(1)}, bf16[256,12,64]{0,2,1:T(8,128)(2,1)}, u32[]{:S(2)}) copy-start(bf16[256,12,64]{0,2,1:T(8,128)(2,1)} %copy-done.5) | copy-start | bytes 1179652
  113.1 2.7 %copy-start.11 = (bf16[12,64,256]{2,1,0:T(8,128)(2,1)S(1)}, bf16[12,64,256]{2,1,0:T(8,128)(2,1)}, u32[]{:S(2)}) copy-start(bf16[12,64,256]{2,1,0:T(8,128)(2,1)} %fusion.40) | copy-start | bytes 1179652
  113.1 3.1 %copy-start.19 = (bf16[768,2304]{1,0:T(8,128)(2,1)S(1)}, bf16[768,2304]{1,0:T(8,128)(2,1)}, u32[]{:S(2)}) copy-start(bf16[768,2304]{1,0:T(8,128)(2,1)} %param.10) | copy-start | bytes 10616836
Sparse Core Ops, SparseCore 0:
  112.5 113.8 reduce-scatter.1
  229.3 23.3 all-reduce.2
where the time goes:
time: 263 us; the launch traced here: 262 us
  waiting for transfers between devices  86.4 us (33%)
  matrix products  83.5 us (32%)
  blocking collectives  43.3 us (16%)
  other arithmetic  19.8 us (8%)
  between operations  14.4 us (5%)
  local copies, waits for them, and re-layouts  11.9 us (5%)
  starting transfers between devices  2.63 us (1%)
    reduce_scatter x1, waiting for transfers between devices, on_device(): shard = lax.psum_scatter(combined, 'seq', scatter_dimension=0, tiled=True)  64.4 us
    psum x1, blocking collectives, on_device(): gain_sum, bias_sum = lax.psum((acc_gain, acc_bias), ('seq', 'slide'))  43.3 us
    dot_general x1, matrix products, attend_back(): jnp.einsum('hqk,qhe->khe', d_scores_b, query, preferred_element_type=jnp....  25.9 us
    dot_general x1, matrix products, attend_back(): jnp.einsum('hqk,khe->qhe', d_scores_b, keys, preferred_element_type=jnp.f...  22.5 us
    psum x1, waiting for transfers between devices, on_device(): shard = lax.psum(shard.astype(jnp.bfloat16), 'slide').astype(jnp.float32)  22.1 us
    concatenate x1, other arithmetic, on_device(): jnp.concatenate([acc_qkv[:, :feature_width], acc_qkv[:, feature_width:] +...  8.74 us
    sub x1, matrix products, attend(): weights = jnp.exp(scores - top)  6.67 us
  transfers between devices with their start and end apart: 3, of which 2 were waited for; matrix products, arithmetic and copies ran while one was open for 7% of the time, Pallas kernels for 0%

commit v1 on v0

--- a/solution.py
+++ b/solution.py
@@ -1,3 +1,4 @@
+import functools
 import jax
 import jax.numpy as jnp
 from jax import lax
@@ -5,6 +6,14 @@
 
 HEADS = 12
 EPS = 1e-05
+
+
+def turn_the_plate(x_in, chip_axis):
+    f_next = jnp.sum(lax.all_gather(x_in, axis_name=chip_axis), axis=0)
+    return f_next
+
+
+work_sections_on = functools.partial(turn_the_plate, chip_axis="slide")
 
 
 def from_behind(block, axis, distance):
@@ -187,7 +196,7 @@
     factor = 1.0 / float(seq_count * slide_count * token_rows.shape[0]) ** 0.5
     gain_sum, bias_sum = lax.psum((acc_gain, acc_bias), ("seq", "slide"))
     shard = lax.psum_scatter(combined, "seq", scatter_dimension=0, tiled=True)
-    shard = lax.psum(shard.astype(jnp.bfloat16), "slide").astype(jnp.float32)
+    shard = work_sections_on(shard.astype(jnp.bfloat16)).astype(jnp.float32)
     shard = shard * factor
     layer_output = block_output[None]
     input_grad = input_gradient[None]

time: 263 us -> 246 us (0.935)
  waiting for transfers between devices: 86.4 us -> 63 us
  blocking collectives: 43.3 us -> 51.5 us
    psum x1 -> x0, waiting for transfers between devices: 22.1 us -> none  [on_device(): shard = lax.psum(shard.astype(jnp.bfloat16), 'slide').astype(jnp.float32)]
    all_gather x0 -> x1, blocking collectives: none -> 9.12 us  [turn_the_plate(): f_next = jnp.sum(lax.all_gather(x_in, axis_name=chip_axis), axis=0)]
  transfers between devices with their start and end apart: 3 -> 2, of which waited for: 2 -> 1; matrix products, arithmetic and copies ran while one was open for 7% -> 8% of each run, Pallas kernels for 0% -> 0%
where the time goes in v1:
time: 246 us; the launch traced here: 245 us
  matrix products  83.5 us (34%)
  waiting for transfers between devices  63 us (26%)
  blocking collectives  51.5 us (21%)
  other arithmetic  18.3 us (7%)
  between operations  14.4 us (6%)
  local copies, waits for them, and re-layouts  11.9 us (5%)
  starting transfers between devices  2.59 us (1%)
    reduce_scatter x1, waiting for transfers between devices, on_device(): shard = lax.psum_scatter(combined, 'seq', scatter_dimension=0, tiled=True)  63 us
    psum x1, blocking collectives, on_device(): gain_sum, bias_sum = lax.psum((acc_gain, acc_bias), ('seq', 'slide'))  42.3 us
    dot_general x1, matrix products, attend_back(): jnp.einsum('hqk,qhe->khe', d_scores_b, query, preferred_element_type=jnp....  25.9 us
    dot_general x1, matrix products, attend_back(): jnp.einsum('hqk,khe->qhe', d_scores_b, keys, preferred_element_type=jnp.f...  22.5 us
    all_gather x1, blocking collectives, turn_the_plate(): f_next = jnp.sum(lax.all_gather(x_in, axis_name=chip_axis), axis=0)  9.12 us
    concatenate x1, other arithmetic, on_device(): jnp.concatenate([acc_qkv[:, :feature_width], acc_qkv[:, feature_width:] +...  8.74 us
    sub x1, matrix products, attend(): weights = jnp.exp(scores - top)  6.67 us
  transfers between devices with their start and end apart: 2, of which 1 were waited for; matrix products, arithmetic and copies ran while one was open for 8% of the time, Pallas kernels for 0%

profile of v1, /device:TPU:0, one launch (start us, length us, event | category | flops | bytes accessed | tf_op | source)
XLA Modules:
  0.0 245.2 jit_solution(12407373695497252435)
XLA Ops:
  7.2 0.0 reduce-scatter.2.cloned.1.call-start
  7.2 2.6 %collective-permute-start = (bf16[256,768]{1,0:T(8,128)(2,1)}, bf16[256,768]{1,0:T(8,128)(2,1)S(1)}, u32[]{:S(2)}, u32[]{:S(2)}) collective-permute-start(bf16[256,768]{1,0:T(8,128)(2,1)} %bitcast.55), channel_id=1, source_target_pairs={{0,2},{2,4},{4,6},{6,8},{8,10},{10,12},{12,14},{14,16},{16,18},{18... | collective-permute-start | bytes 1179656 | tf_op jit(solution)/shard_map/ppermute | solution.py:22
  9.8 1.1 convert_reduce_fusion
  10.9 1.2 fusion.65
  12.2 3.4 %convolution_convert_fusion = bf16[256,2304]{1,0:T(8,128)(2,1)S(1)} fusion(bf16[768,2304]{1,0:T(8,128)(2,1)} %param.10, f32[256]{0:T(256)S(1)} %add_rsqrt_fusion, f32[256]{0:T(256)S(1)} %broadcast_multiply_fusion.4, f32[768]{0:T(1024)} %param.9, f32[768]{0:T(1024)} %param.8, bf16[1,256,768]{2,1,0:T(8,128)(2,1)} %param.6), kind=kOutput, calls=%fused_computation.10 | convolution fusion | flops 907739136 | bytes 5120000 | tf_op jit(solution)/shard_map/dot_general | solution.py:156
  15.6 0.1 fusion.91
  15.7 1.3 convolution_convert_fusion.2
  17.0 0.5 iota_compare_fusion.1
  17.5 1.2 copy.24
  18.6 0.9 copy.22
  19.6 1.4 fusion.69
  21.0 0.1 convert_reduce_fusion.1
  21.1 0.2 fusion.66
  21.4 2.5 %convolution_convert_fusion.1 = bf16[256,1536]{1,0:T(8,128)(2,1)S(1)} fusion(bf16[768,2304]{1,0:T(8,128)(2,1)} %param.10, bf16[256,768]{1,0:T(8,128)(2,1)S(1)} %collective-permute-done, f32[768]{0:T(1024)S(1)} %copy-done.13, f32[768]{0:T(1024)S(1)} %copy-done.12, f32[256]{0:T(256)S(1)} %add_rsqrt_fusion.1, f32[256]{0:T(256)S(1)} %broadcast_multiply_fusion.5), kind=kOutput, calls=%fused_computation.19 | convolution fusion | flops 605552640 | bytes 3547136 | tf_op jit(solution)/shard_map/dot_general | solution.py:164
  24.0 0.1 fusion.94
  24.0 1.3 pad_maximum_fusion.2
  25.3 1.4 copy.21
  26.7 2.3 copy.23
  29.0 6.7 %fusion.95 = (f32[12,256]{1,0:T(8,128)}, f32[12,256,512]{2,1,0:T(8,128)}) fusion(pred[256,512]{1,0:T(8,128)(4,1)} %fusion.69, bf16[256,12,64]{0,2,1:T(8,128)(2,1)S(1)} %bitcast.73, bf16[512,12,64]{0,2,1:T(8,128)(2,1)} %bitcast.71), kind=kOutput, calls=%fused_computation.104 | convolution fusion | flops 207618560 | bytes 7614464 | tf_op jit(solution)/shard_map/sub | solution.py:58
  35.7 4.1 %fusion.37 = bf16[12,64,256]{2,1,0:T(8,128)(2,1)S(1)} fusion(bf16[512,12,64]{0,2,1:T(8,128)(2,1)S(1)} %bitcast.56, f32[12,256,512]{2,1,0:T(8,128)} %get-tuple-element.24, f32[12,256]{1,0:T(8,128)} %get-tuple-element.23), kind=kOutput, calls=%fused_computation.33 | convolution fusion | flops 204668928 | bytes 7483392 | tf_op jit(solution)/shard_map/hqk,khe->qhe/dot_general | solution.py:61
  39.8 0.5 copy-done.20
  40.3 1.7 fusion.30
  42.1 3.7 %fusion.96 = f32[12,256,512]{2,1,0:T(8,128)} fusion(bf16[256,12,64]{0,2,1:T(8,128)(2,1)S(1)} %bitcast.60, bf16[512,12,64]{0,2,1:T(8,128)(2,1)S(1)} %bitcast.57), kind=kOutput, calls=%fused_computation.105 | convolution fusion | flops 201326592 | bytes 7471104 | tf_op jit(solution)/shard_map/qhe,khe->hqk/dot_general | solution.py:69
  45.7 22.5 %fusion.40 = bf16[12,64,256]{2,1,0:T(8,128)(2,1)} fusion(bf16[512,12,64]{0,2,1:T(8,128)(2,1)} %bitcast.72, f32[12,256,512]{2,1,0:T(8,128)} %fusion.96, f32[12,256,512]{2,1,0:T(8,128)} %get-tuple-element.24, f32[12,256]{1,0:T(8,128)} %get-tuple-element.23), kind=kOutput, calls=%fused_computation.34 | convolution fusion | flops 212536832 | bytes 13774848 | tf_op jit(solution)/shard_map/hqk,khe->qhe/dot_general | solution.py:72
  68.2 25.9 %fusion.33 = bf16[512,12,64]{0,2,1:T(8,128)(2,1)} fusion(bf16[256,12,64]{0,2,1:T(8,128)(2,1)S(1)} %bitcast.74, f32[12,256,512]{2,1,0:T(8,128)} %fusion.96, f32[12,256,512]{2,1,0:T(8,128)} %get-tuple-element.24, f32[12,256]{1,0:T(8,128)S(1)} %copy-done.22), kind=kOutput, calls=%fused_computation.30 | convolution fusion | flops 212733440 | bytes 13774848 | tf_op jit(solution)/shard_map/hqk,qhe->khe/dot_general | solution.py:73
  94.1 1.3 fusion.93
  95.4 1.9 fusion.73
  97.3 0.1 fusion.92
  97.4 1.3 fusion.70
  98.8 1.6 slice.80
  100.4 3.3 %slice_add_fusion = f32[768,1536]{1,0:T(8,128)} fusion(f32[768,2304]{1,0:T(8,128)S(1)} %fusion.70, bf16[256,768]{0,1:T(8,128)(2,1)S(1)} %bitcast.61, bf16[256,768]{0,1:T(8,128)(2,1)S(1)} %bitcast.63, bf16[256,768]{1,0:T(8,128)(2,1)S(1)} %collective-permute-done, f32[768]{0:T(1024)S(1)} %copy-done.13, f32[768]{0:T(1024)S(1)} %copy-done.12, ...), kind=kOutput, calls=%fused_computation.9 | convolution fusion | flops 607911936 | bytes 10625024 | tf_op jit(solution)/shard_map/dot_general | solution.py:132
  103.6 8.7 %pad_maximum_fusion = f32[768,3072]{1,0:T(8,128)} fusion(f32[768,768]{1,0:T(8,128)} %fusion.73, f32[768,1536]{1,0:T(8,128)} %slice_add_fusion, f32[768,768]{1,0:T(8,128)} %slice.80), kind=kLoop, calls=%fused_computation.2 | loop fusion | flops 4718592 | bytes 18874368 | tf_op jit(solution)/shard_map/concatenate | solution.py:191
  112.4 0.0 reduce-scatter.2.cloned.1.call-update
  112.4 0.7 copy-done.16
  113.1 2.7 %fusion.90 = (f32[768]{0:T(1024)S(1)}, f32[768]{0:T(1024)S(1)}) fusion(f32[256]{0:T(256)} %copy-done.17, f32[256]{0:T(256)S(1)} %copy-done.16, bf16[256,768]{1,0:T(8,128)(2,1)S(1)} %collective-permute-done, bf16[768,2304]{1,0:T(8,128)(2,1)} %param.10, bf16[256,768]{0,1:T(8,128)(2,1)S(1)} %bitcast.62, bf16[256,768]{0,1:T(8,128)(2,1)S(1)} %bitcast.64), kind=kOutput, calls=%fused_computation.99 | convolution fusion | flops 606730752 | bytes 3547136 | tf_op jit(solution)/shard_map/dot_general | solution.py:135
  115.8 0.4 copy-done.19
  116.1 1.4 fusion.64
  117.6 42.3 %all-reduce = (f32[768]{0:T(1024)S(1)}, f32[768]{0:T(1024)S(1)}) all-reduce(f32[768]{0:T(1024)S(1)} %add.60, f32[768]{0:T(1024)S(1)} %add.61), channel_id=1, replica_groups=mesh['seq'=16,'slide'=2] {'seq','slide'}, use_global_device_ids=true, to_apply=%region_13.14 | all-reduce | flops 1536 | bytes 12288 | tf_op jit(solution)/shard_map/psum | solution.py:197
  159.9 1.3 fusion.43
  161.2 0.6 broadcast_multiply_fusion.1
  161.8 0.6 broadcast_multiply_fusion
  162.4 1.1 fusion.72
  163.4 63.0 %reduce-scatter.2.cloned.1.call-done = f32[48,3072]{1,0:T(8,128)} async-done(((f32[768,3072]{1,0:T(8,128)}), f32[48,3072]{1,0:T(8,128)}) %reduce-scatter.2.cloned.1.call-update) | async-done | bytes 589840 | tf_op jit(solution)/shard_map/reduce_scatter | solution.py:198
  226.4 1.1 convert_element_type.101
  227.5 9.1 %all-gather = bf16[96,3072]{1,0:T(8,128)(2,1)S(1)} all-gather(bf16[48,3072]{1,0:T(8,128)(2,1)S(1)} %convert_element_type.101), channel_id=2, replica_groups=mesh['seq'=16,'slide'=2] {'slide'}, dimensions={0}, use_global_device_ids=true | all-gather | bytes 884736 | tf_op jit(solution)/shard_map/all_gather | solution.py:12
  236.6 0.2 reduce_sum.128
  236.9 0.7 slice.85
  237.6 0.8 slice.84
  (54 shorter events, 0.2 us)
Async XLA Ops:
  7.2 8.5 %copy-start = (bf16[768,768]{1,0:T(8,128)(2,1)S(1)}, bf16[768,768]{1,0:T(8,128)(2,1)}, u32[]{:S(2)}) copy-start(bf16[768,768]{1,0:T(8,128)(2,1)} %param.11) | copy-start | bytes 3538948
  7.2 219.2 %reduce-scatter.2.cloned.1.call-start = ((), (), s32[]{:S(2)}) async-start(), calls=%async_computation.1 | async-start | bytes 10027008 | tf_op jit(solution)/shard_map/reduce_scatter | solution.py:198
  7.2 13.7 %collective-permute-start = (bf16[256,768]{1,0:T(8,128)(2,1)}, bf16[256,768]{1,0:T(8,128)(2,1)S(1)}, u32[]{:S(2)}, u32[]{:S(2)}) collective-permute-start(bf16[256,768]{1,0:T(8,128)(2,1)} %bitcast.55), channel_id=1, source_target_pairs={{0,2},{2,4},{4,6},{6,8},{8,10},{10,12},{12,14},{14,16},{16,18},{18... | collective-permute-start | bytes 1179656 | tf_op jit(solution)/shard_map/ppermute | solution.py:22
  12.2 3.5 %copy-start.2 = (bf16[1,256,768]{2,1,0:T(8,128)(2,1)S(1)}, bf16[1,256,768]{2,1,0:T(8,128)(2,1)}, u32[]{:S(2)}) copy-start(bf16[1,256,768]{2,1,0:T(8,128)(2,1)} %param.7) | copy-start | bytes 1179652
  15.6 5.8 %copy-start.12 = (f32[768]{0:T(1024)S(1)}, f32[768]{0:T(1024)}, u32[]{:S(2)}) copy-start(f32[768]{0:T(1024)} %param.8) | copy-start | bytes 9220
  15.6 5.8 %copy-start.13 = (f32[768]{0:T(1024)S(1)}, f32[768]{0:T(1024)}, u32[]{:S(2)}) copy-start(f32[768]{0:T(1024)} %param.9) | copy-start | bytes 9220
  21.1 2.8 %copy-start.14 = (f32[256]{0:T(256)}, f32[256]{0:T(256)S(1)}, u32[]{:S(2)}) copy-start(f32[256]{0:T(256)S(1)} %broadcast_multiply_fusion.5) | copy-start | bytes 3076
  21.4 2.6 %copy-start.17 = (f32[256]{0:T(256)}, f32[256]{0:T(256)S(1)}, u32[]{:S(2)}) copy-start(f32[256]{0:T(256)S(1)} %add_rsqrt_fusion.1) | copy-start | bytes 3076
  24.0 5.0 %copy-start.8 = (bf16[256,768]{0,1:T(8,128)(2,1)S(1)}, bf16[256,768]{0,1:T(8,128)(2,1)}, u32[]{:S(2)}) copy-start(bf16[256,768]{0,1:T(8,128)(2,1)} %copy.22) | copy-start | bytes 1179652
  35.7 4.6 %copy-start.20 = (f32[12,256,512]{2,1,0:T(8,128)S(1)}, f32[12,256,512]{2,1,0:T(8,128)}, u32[]{:S(2)}) copy-start(f32[12,256,512]{2,1,0:T(8,128)} %get-tuple-element.24) | copy-start | bytes 18874372
  35.7 4.6 %copy-start.21 = (f32[12,256]{1,0:T(8,128)S(1)}, f32[12,256]{1,0:T(8,128)}, u32[]{:S(2)}) copy-start(f32[12,256]{1,0:T(8,128)} %get-tuple-element.23) | copy-start | bytes 36868
  45.7 22.5 %copy-start.9 = (bf16[256,768]{0,1:T(8,128)(2,1)S(1)}, bf16[256,768]{0,1:T(8,128)(2,1)}, u32[]{:S(2)}) copy-start(bf16[256,768]{0,1:T(8,128)(2,1)} %copy.22) | copy-start | bytes 1179652
  45.7 22.5 %copy-start.22 = (f32[12,256]{1,0:T(8,128)S(1)}, f32[12,256]{1,0:T(8,128)}, u32[]{:S(2)}) copy-start(f32[12,256]{1,0:T(8,128)} %get-tuple-element.23) | copy-start | bytes 36868
  94.1 3.2 %copy-start.7 = (bf16[512,12,64]{0,2,1:T(8,128)(2,1)S(1)}, bf16[512,12,64]{0,2,1:T(8,128)(2,1)}, u32[]{:S(2)}) copy-start(bf16[512,12,64]{0,2,1:T(8,128)(2,1)} %fusion.33) | copy-start | bytes 2359300
  94.1 3.3 %copy-start.1 = (bf16[1,256,768]{2,1,0:T(8,128)(2,1)S(1)}, bf16[1,256,768]{2,1,0:T(8,128)(2,1)}, u32[]{:S(2)}) copy-start(bf16[1,256,768]{2,1,0:T(8,128)(2,1)} %param.6) | copy-start | bytes 1179652
  94.1 3.3 %copy-start.10 = (bf16[12,64,256]{2,1,0:T(8,128)(2,1)S(1)}, bf16[12,64,256]{2,1,0:T(8,128)(2,1)}, u32[]{:S(2)}) copy-start(bf16[12,64,256]{2,1,0:T(8,128)(2,1)} %fusion.40) | copy-start | bytes 1179652
  95.4 3.3 %copy-start.3 = (bf16[256,12,64]{0,2,1:T(8,128)(2,1)}, bf16[256,12,64]{0,2,1:T(8,128)(2,1)S(1)}, u32[]{:S(2)}) copy-start(bf16[256,12,64]{0,2,1:T(8,128)(2,1)S(1)} %get-tuple-element.20) | copy-start | bytes 1179652
  97.4 1.4 copy-start.5
  98.8 1.6 copy-start.15
  98.8 1.6 copy-start.18
  112.4 0.7 copy-start.16
  113.0 2.7 %copy-start.4 = (bf16[256,12,64]{0,2,1:T(8,128)(2,1)S(1)}, bf16[256,12,64]{0,2,1:T(8,128)(2,1)}, u32[]{:S(2)}) copy-start(bf16[256,12,64]{0,2,1:T(8,128)(2,1)} %copy-done.3) | copy-start | bytes 1179652
  113.1 2.7 %copy-start.6 = (bf16[256,12,64]{0,2,1:T(8,128)(2,1)S(1)}, bf16[256,12,64]{0,2,1:T(8,128)(2,1)}, u32[]{:S(2)}) copy-start(bf16[256,12,64]{0,2,1:T(8,128)(2,1)} %copy-done.5) | copy-start | bytes 1179652
  113.1 2.7 %copy-start.11 = (bf16[12,64,256]{2,1,0:T(8,128)(2,1)S(1)}, bf16[12,64,256]{2,1,0:T(8,128)(2,1)}, u32[]{:S(2)}) copy-start(bf16[12,64,256]{2,1,0:T(8,128)(2,1)} %fusion.40) | copy-start | bytes 1179652
  113.1 3.1 %copy-start.19 = (bf16[768,2304]{1,0:T(8,128)(2,1)S(1)}, bf16[768,2304]{1,0:T(8,128)(2,1)}, u32[]{:S(2)}) copy-start(bf16[768,2304]{1,0:T(8,128)(2,1)} %param.10) | copy-start | bytes 10616836
Sparse Core Ops, SparseCore 0:
  112.5 113.8 reduce-scatter.1
